TPU v7x, 128 devices: a whole 4x4x4 slice. The times are simulated.
128 devices in a mesh: vocab: 32 (over x, z, core), group: 4 (over y).
Axes of the slice: x: 4, y: 4, z: 4, core: 2. Of those that a mesh axis runs over, the one named last changes fastest.
Arguments:
- hidden_states: bfloat16 [2048, 4096], P(('group', 'vocab')), parts along dimension 0, may hold values from -32 to 32
- head_weight: bfloat16 [4096, 77824], P(None, 'vocab'), may hold values from -1 to 1
- pick_index: int32 [2048, 64], P('group'), parts along dimension 0, may hold values from 0 to 77823, as said below
- owner_order: int32 [2048], P('group'), parts along dimension 0, may hold values from 0 to 511, each once
Outputs:
- token_logprobs: float32 [2048, 64], P(('group', 'vocab')), parts along dimension 0
- token_logtotal: float32 [2048], P(('group', 'vocab')), parts along dimension 0
There are 4 independent parts, one for each index of `group`. A program takes and returns all parts, laid end to end along the dimension named above; an argument that names none is the same for every part. Nothing has to cross between parts.
Inputs may be any that keep to these rules, and one draw needn't show every extreme that they name: `pick_index`: each row holds 64 distinct vocabulary entries. `owner_order`: each token appears once.
All inputs are finite; a program needn't handle non-finite values.
Results may differ from a plain program's by a relative error of at most 0.0003.
Values may be sent and summed in bfloat16 or wider, within the bound.
A program may use at most 128 MiB of HBM per device.

v0:
```python
import math

import jax
import jax.numpy as jnp
from jax import lax
from jax.sharding import PartitionSpec as P


def sent_together(arrays, axis, split_dim, concat_dim, along):
    widths = [math.prod(a.shape[along:]) for a in arrays]
    both = jnp.concatenate(
        [a.reshape(*a.shape[:along], w) for a, w in zip(arrays, widths)], axis=along
    )
    filled = lax.all_to_all(both, axis, split_axis=split_dim, concat_axis=concat_dim, tiled=True)
    tiles = jnp.split(filled, [sum(widths[:k]) for k in range(1, len(widths))], axis=along)
    return tuple(
        (b.reshape(*filled.shape[:along], *a.shape[along:]) for a, b in zip(arrays, tiles))
    )


def select_block(pair):
    block_logits, block_index = pair
    columns = lax.broadcasted_iota(jnp.int32, (1, 1, block_logits.shape[1]), 2)
    matches = block_index[:, :, None] == columns
    return jnp.sum(jnp.where(matches, block_logits[:, None, :], 0.0), axis=2)


def local(hidden_states, head_weight, pick_index, owner_order):
    shard_count = lax.axis_size("vocab")
    shard_width = head_weight.shape[1]
    shard_index = lax.axis_index("vocab")
    shard_start = shard_index * shard_width
    own_rows = hidden_states.shape[0]
    pick_count = pick_index.shape[1]
    all_rows = pick_index.shape[0]
    logits = jnp.dot(
        lax.all_gather(hidden_states, "vocab", axis=0, tiled=True),
        head_weight,
        preferred_element_type=jnp.float32,
    )
    local_index = pick_index - shard_start
    block_size = math.gcd(all_rows, 32)
    block_count = all_rows // block_size
    picked = lax.map(
        select_block,
        (
            logits.reshape(block_count, block_size, shard_width),
            local_index.reshape(block_count, block_size, pick_count),
        ),
    )
    picked = picked.reshape(all_rows, pick_count)
    picked = jnp.take(picked, owner_order, axis=0)
    local_max = jnp.max(logits, axis=1)
    local_sum = jnp.sum(jnp.exp(logits - local_max[:, None]), axis=1)
    sent_max = jnp.take(local_max, owner_order, axis=0).reshape(shard_count, own_rows)
    sent_sum = jnp.take(local_sum, owner_order, axis=0).reshape(shard_count, own_rows)
    sent_picks = picked.reshape(shard_count, own_rows, pick_count)
    received_picks, maxima, totals = sent_together(
        (sent_picks, sent_max, sent_sum), "vocab", 0, 0, 2
    )
    overall_max = jnp.max(maxima, axis=0)
    log_total = overall_max + jnp.log(
        jnp.sum(totals * jnp.exp(maxima - overall_max[None, :]), axis=0)
    )
    logprobs = jnp.sum(received_picks, axis=0) - log_total[:, None]
    return (logprobs, log_total)


def solution(mesh):
    in_specs = (P(("group", "vocab"), None), P(None, "vocab"), P("group", None), P("group"))
    out_specs = (P(("group", "vocab"), None), P(("group", "vocab")))
    return jax.shard_map(local, mesh=mesh, in_specs=in_specs, out_specs=out_specs, check_vma=False)
```

profile of v0, /device:TPU:1, one launch (start us, length us, event | category | flops | bytes accessed | tf_op | source)
XLA Modules:
  0.0 171.2 jit_solution(4934463878502503390)
XLA Ops:
  7.2 0.0 all-gather.2.cloned.1.call-start
  7.2 0.7 all-gather.2.cloned.1.call-update
  7.9 0.9 broadcast_subtract_fusion
  8.8 0.1 copy.20
  9.0 0.7 compare_select_fusion
  9.7 50.4 %all-gather.2.cloned.1.call-done = bf16[512,4096]{1,0:T(8,128)(2,1)} async-done(((bf16[16,4096]{1,0:T(8,128)(2,1)}), bf16[512,4096]{1,0:T(8,128)(2,1)}) %all-gather.2.cloned.1.call-update) | async-done | bytes 4194320 | tf_op jit(solution)/shard_map/all_gather | solution.py:37
  60.0 16.3 %fusion.4 = (f32[512]{0:T(512)S(1)}, f32[512,2432]{1,0:T(8,128)S(1)}) fusion(bf16[512,4096]{1,0:T(8,128)(2,1)} %all-gather.2.cloned.1.call-done, bf16[4096,2432]{1,0:T(8,128)(2,1)} %param.9), kind=kOutput, calls=%fused_computation.26 | convolution fusion | flops 10201792512 | bytes 29100032 | tf_op jit(solution)/shard_map/dot_general | solution.py:36
  76.3 0.0 copy-start
  76.3 0.0 copy-start.1
  76.4 2.2 %copy-done = f32[512,2432]{1,0:T(8,128)} copy-done((f32[512,2432]{1,0:T(8,128)}, f32[512,2432]{1,0:T(8,128)S(1)}, u32[]{:S(2)}) %copy-start) | copy-done | bytes 4980760
  78.5 0.8 exponential_reduce_fusion
  79.3 3.5 %gather_fusion.1 = f32[512]{0:T(512)S(1)} fusion(f32[512]{0:T(512)S(1)} %get-tuple-element.43, s32[1024]{0:T(1024)S(1)} %pad_clamp_fusion), kind=kCustom, calls=%fused_computation.clone | custom fusion | bytes 6144 | tf_op jit(solution)/shard_map/jit(_take)/gather | solution.py:55
  82.8 3.5 %gather_fusion.2 = f32[512]{0:T(512)S(1)} fusion(f32[512]{0:T(512)S(1)} %exponential_reduce_fusion, s32[1024]{0:T(1024)S(1)} %pad_clamp_fusion), kind=kCustom, calls=%fused_computation.1.clone | custom fusion | bytes 6144 | tf_op jit(solution)/shard_map/jit(_take)/gather | solution.py:56
  86.3 0.0 copy-done.1
  86.4 0.1 broadcast_in_dim.46
  86.5 0.2 reshape_reshape.9
  86.7 60.4 %while.10 = (s32[]{:T(128)}, f32[16,32,64]{2,1,0:T(8,128)S(1)}, s32[16,32,64]{2,1,0:T(8,128)S(1)}, f32[16,32,2432]{2,1,0:T(8,128)}, s32[]{:T(128)}) while((s32[]{:T(128)}, f32[16,32,64]{2,1,0:T(8,128)S(1)}, s32[16,32,64]{2,1,0:T(8,128)S(1)}, f32[16,32,2432]{2,1,0:T(8,128)}, s32[]{:T(128)}) %tuple.35), condition=%wide.region_2.3_spmd, body=%wide.region_0.2_spmd.sunk | while | flops 14940162 | bytes 999497 | solution.py:44
  86.7 1.0 dynamic-slice_bitcast_fusion.4
  87.7 2.7 %select_reduce_fusion.2 = f32[32,64]{1,0:T(8,128)S(1)} fusion(f32[32,2432]{1,0:T(8,128)S(1)} %dynamic-slice_bitcast_fusion.4, s32[32,64]{1,0:T(8,128)S(1)} %dynamic-slice_bitcast_fusion.5), kind=kLoop, calls=%fused_computation.3.clone.1 | loop fusion | flops 14940160 | bytes 327680 | tf_op jit(solution)/shard_map/while/body/eval_jaxpr/reduce_sum | solution.py:25
  90.5 1.0 dynamic-slice_bitcast_fusion.4
  91.5 2.7 %select_reduce_fusion.2 = f32[32,64]{1,0:T(8,128)S(1)} fusion(f32[32,2432]{1,0:T(8,128)S(1)} %dynamic-slice_bitcast_fusion.4, s32[32,64]{1,0:T(8,128)S(1)} %dynamic-slice_bitcast_fusion.5), kind=kLoop, calls=%fused_computation.3.clone.1 | loop fusion | flops 14940160 | bytes 327680 | tf_op jit(solution)/shard_map/while/body/eval_jaxpr/reduce_sum | solution.py:25
  94.2 1.0 dynamic-slice_bitcast_fusion.4
  95.2 2.7 %select_reduce_fusion.2 = f32[32,64]{1,0:T(8,128)S(1)} fusion(f32[32,2432]{1,0:T(8,128)S(1)} %dynamic-slice_bitcast_fusion.4, s32[32,64]{1,0:T(8,128)S(1)} %dynamic-slice_bitcast_fusion.5), kind=kLoop, calls=%fused_computation.3.clone.1 | loop fusion | flops 14940160 | bytes 327680 | tf_op jit(solution)/shard_map/while/body/eval_jaxpr/reduce_sum | solution.py:25
  98.0 1.0 dynamic-slice_bitcast_fusion.4
  99.0 2.7 %select_reduce_fusion.2 = f32[32,64]{1,0:T(8,128)S(1)} fusion(f32[32,2432]{1,0:T(8,128)S(1)} %dynamic-slice_bitcast_fusion.4, s32[32,64]{1,0:T(8,128)S(1)} %dynamic-slice_bitcast_fusion.5), kind=kLoop, calls=%fused_computation.3.clone.1 | loop fusion | flops 14940160 | bytes 327680 | tf_op jit(solution)/shard_map/while/body/eval_jaxpr/reduce_sum | solution.py:25
  101.8 1.0 dynamic-slice_bitcast_fusion.4
  102.8 2.7 %select_reduce_fusion.2 = f32[32,64]{1,0:T(8,128)S(1)} fusion(f32[32,2432]{1,0:T(8,128)S(1)} %dynamic-slice_bitcast_fusion.4, s32[32,64]{1,0:T(8,128)S(1)} %dynamic-slice_bitcast_fusion.5), kind=kLoop, calls=%fused_computation.3.clone.1 | loop fusion | flops 14940160 | bytes 327680 | tf_op jit(solution)/shard_map/while/body/eval_jaxpr/reduce_sum | solution.py:25
  105.6 1.0 dynamic-slice_bitcast_fusion.4
  106.6 2.7 %select_reduce_fusion.2 = f32[32,64]{1,0:T(8,128)S(1)} fusion(f32[32,2432]{1,0:T(8,128)S(1)} %dynamic-slice_bitcast_fusion.4, s32[32,64]{1,0:T(8,128)S(1)} %dynamic-slice_bitcast_fusion.5), kind=kLoop, calls=%fused_computation.3.clone.1 | loop fusion | flops 14940160 | bytes 327680 | tf_op jit(solution)/shard_map/while/body/eval_jaxpr/reduce_sum | solution.py:25
  109.3 1.0 dynamic-slice_bitcast_fusion.4
  110.3 2.7 %select_reduce_fusion.2 = f32[32,64]{1,0:T(8,128)S(1)} fusion(f32[32,2432]{1,0:T(8,128)S(1)} %dynamic-slice_bitcast_fusion.4, s32[32,64]{1,0:T(8,128)S(1)} %dynamic-slice_bitcast_fusion.5), kind=kLoop, calls=%fused_computation.3.clone.1 | loop fusion | flops 14940160 | bytes 327680 | tf_op jit(solution)/shard_map/while/body/eval_jaxpr/reduce_sum | solution.py:25
  113.1 1.0 dynamic-slice_bitcast_fusion.4
  114.1 2.7 %select_reduce_fusion.2 = f32[32,64]{1,0:T(8,128)S(1)} fusion(f32[32,2432]{1,0:T(8,128)S(1)} %dynamic-slice_bitcast_fusion.4, s32[32,64]{1,0:T(8,128)S(1)} %dynamic-slice_bitcast_fusion.5), kind=kLoop, calls=%fused_computation.3.clone.1 | loop fusion | flops 14940160 | bytes 327680 | tf_op jit(solution)/shard_map/while/body/eval_jaxpr/reduce_sum | solution.py:25
  116.9 1.0 dynamic-slice_bitcast_fusion.4
  117.9 2.7 %select_reduce_fusion.2 = f32[32,64]{1,0:T(8,128)S(1)} fusion(f32[32,2432]{1,0:T(8,128)S(1)} %dynamic-slice_bitcast_fusion.4, s32[32,64]{1,0:T(8,128)S(1)} %dynamic-slice_bitcast_fusion.5), kind=kLoop, calls=%fused_computation.3.clone.1 | loop fusion | flops 14940160 | bytes 327680 | tf_op jit(solution)/shard_map/while/body/eval_jaxpr/reduce_sum | solution.py:25
  120.6 1.0 dynamic-slice_bitcast_fusion.4
  121.7 2.7 %select_reduce_fusion.2 = f32[32,64]{1,0:T(8,128)S(1)} fusion(f32[32,2432]{1,0:T(8,128)S(1)} %dynamic-slice_bitcast_fusion.4, s32[32,64]{1,0:T(8,128)S(1)} %dynamic-slice_bitcast_fusion.5), kind=kLoop, calls=%fused_computation.3.clone.1 | loop fusion | flops 14940160 | bytes 327680 | tf_op jit(solution)/shard_map/while/body/eval_jaxpr/reduce_sum | solution.py:25
  124.4 1.0 dynamic-slice_bitcast_fusion.4
  125.4 2.7 %select_reduce_fusion.2 = f32[32,64]{1,0:T(8,128)S(1)} fusion(f32[32,2432]{1,0:T(8,128)S(1)} %dynamic-slice_bitcast_fusion.4, s32[32,64]{1,0:T(8,128)S(1)} %dynamic-slice_bitcast_fusion.5), kind=kLoop, calls=%fused_computation.3.clone.1 | loop fusion | flops 14940160 | bytes 327680 | tf_op jit(solution)/shard_map/while/body/eval_jaxpr/reduce_sum | solution.py:25
  128.2 1.0 dynamic-slice_bitcast_fusion.4
  129.2 2.7 %select_reduce_fusion.2 = f32[32,64]{1,0:T(8,128)S(1)} fusion(f32[32,2432]{1,0:T(8,128)S(1)} %dynamic-slice_bitcast_fusion.4, s32[32,64]{1,0:T(8,128)S(1)} %dynamic-slice_bitcast_fusion.5), kind=kLoop, calls=%fused_computation.3.clone.1 | loop fusion | flops 14940160 | bytes 327680 | tf_op jit(solution)/shard_map/while/body/eval_jaxpr/reduce_sum | solution.py:25
  132.0 1.0 dynamic-slice_bitcast_fusion.4
  133.0 2.7 %select_reduce_fusion.2 = f32[32,64]{1,0:T(8,128)S(1)} fusion(f32[32,2432]{1,0:T(8,128)S(1)} %dynamic-slice_bitcast_fusion.4, s32[32,64]{1,0:T(8,128)S(1)} %dynamic-slice_bitcast_fusion.5), kind=kLoop, calls=%fused_computation.3.clone.1 | loop fusion | flops 14940160 | bytes 327680 | tf_op jit(solution)/shard_map/while/body/eval_jaxpr/reduce_sum | solution.py:25
  135.7 1.0 dynamic-slice_bitcast_fusion.4
  136.7 2.7 %select_reduce_fusion.2 = f32[32,64]{1,0:T(8,128)S(1)} fusion(f32[32,2432]{1,0:T(8,128)S(1)} %dynamic-slice_bitcast_fusion.4, s32[32,64]{1,0:T(8,128)S(1)} %dynamic-slice_bitcast_fusion.5), kind=kLoop, calls=%fused_computation.3.clone.1 | loop fusion | flops 14940160 | bytes 327680 | tf_op jit(solution)/shard_map/while/body/eval_jaxpr/reduce_sum | solution.py:25
  139.5 1.0 dynamic-slice_bitcast_fusion.4
  140.5 2.7 %select_reduce_fusion.2 = f32[32,64]{1,0:T(8,128)S(1)} fusion(f32[32,2432]{1,0:T(8,128)S(1)} %dynamic-slice_bitcast_fusion.4, s32[32,64]{1,0:T(8,128)S(1)} %dynamic-slice_bitcast_fusion.5), kind=kLoop, calls=%fused_computation.3.clone.1 | loop fusion | flops 14940160 | bytes 327680 | tf_op jit(solution)/shard_map/while/body/eval_jaxpr/reduce_sum | solution.py:25
  143.3 1.0 dynamic-slice_bitcast_fusion.4
  144.3 2.7 %select_reduce_fusion.2 = f32[32,64]{1,0:T(8,128)S(1)} fusion(f32[32,2432]{1,0:T(8,128)S(1)} %dynamic-slice_bitcast_fusion.4, s32[32,64]{1,0:T(8,128)S(1)} %dynamic-slice_bitcast_fusion.5), kind=kLoop, calls=%fused_computation.3.clone.1 | loop fusion | flops 14940160 | bytes 327680 | tf_op jit(solution)/shard_map/while/body/eval_jaxpr/reduce_sum | solution.py:25
  147.0 1.0 gather_fusion
  148.1 0.2 reshape_reshape.8
  148.3 0.1 broadcast_select_fusion
  148.4 0.2 pad_maximum_fusion
  148.6 14.1 %all_to_all.5 = f32[32,16,66]{2,1,0:T(8,128)S(1)} all-to-all(f32[32,16,66]{2,1,0:T(8,128)S(1)} %pad_maximum_fusion), channel_id=1, replica_groups=mesh['vocab'=32,'group'=4] {'vocab'}, dimensions={0} | all-to-all | bytes 270336 | tf_op jit(solution)/shard_map/all_to_all | solution.py:14
  162.7 0.3 fusion.3
  163.0 0.2 copy.28
  163.2 0.2 copy.29
  163.4 0.2 fusion.2
  163.6 0.0 copy-start.2
  163.6 0.1 copy.27
  163.7 0.7 copy.26
  164.4 0.0 copy-done.2
  (39 shorter events, 0.3 us)
Async XLA Ops:
  7.2 52.9 %all-gather.2.cloned.1.call-start = ((), (), s32[]{:S(2)}) async-start(), calls=%async_computation.1 | async-start | bytes 4325376 | tf_op jit(solution)/shard_map/all_gather | solution.py:37
  76.3 2.2 %copy-start = (f32[512,2432]{1,0:T(8,128)}, f32[512,2432]{1,0:T(8,128)S(1)}, u32[]{:S(2)}) copy-start(f32[512,2432]{1,0:T(8,128)S(1)} %get-tuple-element.44) | copy-start | bytes 14942212
  76.3 10.0 %copy-start.1 = (s32[512]{0:T(512)S(1)}, s32[512]{0:T(512)}, u32[]{:S(2)}) copy-start(s32[512]{0:T(512)} %param.11) | copy-start | bytes 6148
  163.6 0.8 copy-start.2
Sparse Core Ops, SparseCore 0:
  10.2 49.7 all-gather.1
where the time goes:
time: 172 us; the launch traced here: 171 us
  waiting for transfers between devices  51 us (30%)
  other arithmetic  47.3 us (28%)
  local copies, waits for them, and re-layouts  28.1 us (16%)
  matrix products  16.3 us (9%)
  between operations  14.2 us (8%)
  blocking collectives  14.1 us (8%)
    all_gather x1, waiting for transfers between devices, local(): lax.all_gather(hidden_states, 'vocab', axis=0, tiled=True)  50.4 us
    reduce_sum x16, other arithmetic, select_block(): return jnp.sum(jnp.where(matches, block_logits[:, None, :], 0.0), axis=2)  44 us
    dot_general x1, matrix products, local(): jnp.dot(lax.all_gather(hidden_states, 'vocab', axis=0, tiled=True), head_...  16.3 us
    broadcast_in_dim x16, local copies, waits for them, and re-layouts, select_block(): return jnp.sum(jnp.where(matches, block_logits[:, None, :], 0.0), axis=2)  15.9 us
    all_to_all x1, blocking collectives, sent_together(): lax.all_to_all(both, axis, split_axis=split_dim, concat_axis=concat_dim,...  14.1 us
    gather x1, local copies, waits for them, and re-layouts, local(): jnp.take(local_sum, owner_order, axis=0).reshape(shard_count, own_rows)  3.49 us
    gather x1, local copies, waits for them, and re-layouts, local(): jnp.take(local_max, owner_order, axis=0).reshape(shard_count, own_rows)  3.49 us
  transfers between devices with their start and end apart: 1, of which 1 were waited for; matrix products, arithmetic and copies ran while one was open for 1% of the time, Pallas kernels for 0%

commit v1 on v0

v1 whole, which is shorter than its diff:
```python
import functools

import jax
import jax.numpy as jnp
from jax import lax
from jax.experimental import pallas as pl
from jax.experimental.pallas import tpu as pltpu
from jax.sharding import PartitionSpec as P

MESH = pl.DeviceIdType.MESH
SIDE = 4
SHARDS = 2 * SIDE * SIDE
LANES = 128
TILE = 512
BLOCKS = 4
PLACE = {
    (0, 0): (0, 0), (3, 0): (0, 1), (1, 0): (0, 2), (0, 1): (0, 3),
    (0, 3): (1, 0), (2, 0): (1, 1), (3, 1): (1, 2), (3, 3): (1, 3),
    (1, 1): (2, 0), (1, 3): (2, 1), (2, 1): (2, 2), (2, 3): (2, 3),
    (0, 2): (3, 0), (3, 2): (3, 1), (1, 2): (3, 2), (2, 2): (3, 3),
}
HALVED = ((2, 0), (0, 2), (3, 2), (1, 2), (2, 2))
WHOLE = tuple(rel for rel in PLACE if rel not in HALVED and rel != (0, 0))
ARRIVALS = [(rel, None) for rel in WHOLE] + [(rel, half) for rel in HALVED for half in (0, 1)]
RECV = {key: number for number, key in enumerate(ARRIVALS)}
SENDS = 40


def flat(x, z, core):
    return ((x % SIDE) * SIDE + z % SIDE) * 2 + core


def kernel(
    x_ref, w_ref, pick_ref, order_ref, logp_ref, total_ref,
    hidden, weight, logits, top, mass, found, low, high, pieces, perm, outbox, inbox,
    own_sem, weight_sem, send_sem, recv_sem, pair_sem, out_sem, in_sem,
):
    rows, depth = x_ref.shape
    width = w_ref.shape[1]
    tokens, picks = pick_ref.shape
    half_depth = depth // 2
    chunk_rows = 2 * BLOCKS * rows
    tiles = [(start, min(TILE, width - start)) for start in range(0, width, TILE)]

    me = lax.axis_index("vocab")
    core = me % 2
    x = me // 2 // SIDE
    z = me // 2 % SIDE
    pair = me + 1 - 2 * core

    def at(da, db, kind):
        return (1 - kind) * flat(x + da, z + db, kind) + kind * flat(x + db, z + da, kind)

    first_up, first_down = at(1, 0, core), at(3, 0, core)
    second_up, second_down = at(0, 1, core), at(0, 3, core)

    def block(rel, half=None, other=0):
        chunk, slot = PLACE[rel]
        row = (slot + BLOCKS * other) * rows
        if half is None:
            return hidden.at[chunk, pl.ds(row, rows), :]
        return hidden.at[chunk, pl.ds(row, rows), pl.ds(half * half_depth, half_depth)]

    own_copy = pltpu.make_async_copy(x_ref, block((0, 0)), own_sem)
    own_copy.start()
    weight_copies = []
    for number, (start, size) in enumerate(tiles):
        copy = pltpu.make_async_copy(
            w_ref.at[:, pl.ds(start, size)], weight.at[:, pl.ds(start, size)], weight_sem.at[number]
        )
        copy.start()
        weight_copies.append(copy)

    barrier = pltpu.get_barrier_semaphore()
    for partner in (first_up, first_down, second_up, second_down, pair):
        pl.semaphore_signal(barrier, inc=1, device_id={"vocab": partner}, device_id_type=MESH)

    order = jnp.broadcast_to(order_ref[...].astype(jnp.float32), (LANES, tokens))
    order = jnp.transpose(order)
    lanes = lax.broadcasted_iota(jnp.int32, (tokens, LANES), 1).astype(jnp.float32)
    for start in range(0, tokens, LANES):
        perm[:, pl.ds(start, LANES)] = jnp.where(order == lanes + start, 1.0, 0.0).astype(jnp.bfloat16)
    places = pick_ref[...] - me * width
    places = jnp.concatenate([places, places], axis=1)
    low[...] = places & (LANES - 1)
    high[...] = places >> 7

    own_copy.wait()
    pl.semaphore_wait(barrier, 5)

    started = []

    def push(src, dst, recv, to):
        copy = pltpu.make_async_remote_copy(
            src_ref=src, dst_ref=dst, send_sem=send_sem.at[len(started)], recv_sem=recv,
            device_id={"vocab": to}, device_id_type=MESH,
        )
        copy.start()
        started.append(copy)

    def arrived(rel, half=None):
        ref = block(rel, half)
        pltpu.make_async_remote_copy(
            src_ref=ref, dst_ref=ref, send_sem=send_sem.at[0], recv_sem=recv_sem.at[RECV[rel, half]],
            device_id={"vocab": pair}, device_id_type=MESH,
        ).wait_recv()

    def across(rel, to_rel, to, half=None):
        push(block(rel, half), block(to_rel, half), recv_sem.at[RECV[to_rel, half]], to)

    def to_pair(rel):
        push(block(rel), block(rel, other=1), pair_sem.at[PLACE[rel][0]], pair)

    def along_second(rel):
        across(rel, (rel[0], 3), second_up)
        across(rel, (rel[0], 1), second_down)

    def service(rel):
        if rel in HALVED:
            arrived(rel, 0)
            arrived(rel, 1)
        else:
            arrived(rel)
        if rel == (3, 0):
            across(rel, (2, 0), first_up, 0)
        if rel == (1, 0):
            across(rel, (2, 0), first_down, 1)
        if rel[1] == 0:
            along_second(rel)
        if rel[1] == 3:
            across(rel, (rel[0], 2), second_up, 0)
        if rel[1] == 1:
            across(rel, (rel[0], 2), second_down, 1)
        to_pair(rel)

    def pair_arrived(chunk):
        ref = hidden.at[chunk, pl.ds(BLOCKS * rows, BLOCKS * rows), :]
        pltpu.make_async_remote_copy(
            src_ref=ref, dst_ref=ref, send_sem=send_sem.at[0], recv_sem=pair_sem.at[chunk],
            device_id={"vocab": pair}, device_id_type=MESH,
        ).wait_recv()

    across((0, 0), (3, 0), first_up)
    across((0, 0), (1, 0), first_down)
    along_second((0, 0))
    to_pair((0, 0))
    for rel in ((3, 0), (1, 0), (0, 1), (0, 3)):
        service(rel)

    services = {
        (0, 1): ((2, 0),), (0, 3): ((3, 3), (3, 1)),
        (1, 1): ((1, 1), (1, 3)), (1, 3): ((2, 1), (2, 3)),
        (2, 1): ((0, 2), (3, 2)), (2, 3): ((1, 2), (2, 2)),
    }

    def positions(chunk):
        spots = [None] * (2 * BLOCKS)
        for rel, (number, slot) in PLACE.items():
            if number == chunk:
                spots[slot] = at(*rel, core)
                spots[slot + BLOCKS] = at(*rel, 1 - core)
        return [pl.multiple_of(spot * rows, rows) for spot in spots]

    def digest(chunk, number, spots):
        start, size = tiles[number]
        first = start // LANES
        values = [logits[:, pl.ds(start + LANES * k, LANES)] for k in range(size // LANES)]
        best = functools.reduce(jnp.maximum, values)
        if number == 0:
            total = jnp.zeros_like(best)
            chosen = jnp.zeros_like(best)
        else:
            old = top[...]
            best = jnp.maximum(best, old)
            total = mass[...] * jnp.exp(old - best)
            chosen = found[...]
        lane = jnp.concatenate([low[pl.ds(spot, rows), :] for spot in spots], axis=0)
        tile = jnp.concatenate([high[pl.ds(spot, rows), :] for spot in spots], axis=0)
        for k, value in enumerate(values):
            total = total + jnp.exp(value - best)
            taken = jnp.take_along_axis(value, lane, axis=1, mode="promise_in_bounds")
            chosen = jnp.where(tile == first + k, taken, chosen)
        top[...] = best
        mass[...] = total
        found[...] = chosen

    for chunk in range(4):
        pair_arrived(chunk)
        spots = positions(chunk)
        for number, (start, size) in enumerate(tiles):
            if chunk == 0:
                weight_copies[number].wait()
            logits[:, pl.ds(start, size)] = jnp.dot(
                hidden[chunk], weight[:, pl.ds(start, size)], preferred_element_type=jnp.float32
            )
            if number > 0:
                digest(chunk, number - 1, spots)
            for rel in services.get((chunk, number), ()):
                service(rel)
        digest(chunk, len(tiles) - 1, spots)
        peak = jnp.max(top[...], axis=1, keepdims=True)
        lse = peak + jnp.log(jnp.sum(mass[...] * jnp.exp(top[...] - peak), axis=1, keepdims=True))
        lane = lax.broadcasted_iota(jnp.int32, (chunk_rows, LANES), 1)
        rest = jnp.where(lane < picks, found[...], lse)
        parts = []
        for _ in range(3):
            part = rest.astype(jnp.bfloat16)
            rest = rest - part.astype(jnp.float32)
            parts.append(part)
        parts = jnp.concatenate(parts, axis=1)
        for k, spot in enumerate(spots):
            pieces[pl.ds(spot, rows), :] = parts[k * rows : (k + 1) * rows]

    sorted_parts = jnp.dot(perm[...], pieces[...], preferred_element_type=jnp.float32)
    outbox[...] = (sorted_parts[:, :LANES] + sorted_parts[:, LANES : 2 * LANES]) + sorted_parts[:, 2 * LANES :]

    for step in range(1, SHARDS):
        owner = (me + step) % SHARDS
        pltpu.make_async_remote_copy(
            src_ref=outbox.at[pl.ds(pl.multiple_of(owner * rows, rows), rows), :], dst_ref=inbox.at[step - 1],
            send_sem=out_sem, recv_sem=in_sem, device_id={"vocab": owner}, device_id_type=MESH,
        ).start()
    for copy in started:
        copy.wait_send()
    everything = pltpu.make_async_remote_copy(
        src_ref=inbox, dst_ref=inbox, send_sem=out_sem, recv_sem=in_sem,
        device_id={"vocab": pair}, device_id_type=MESH,
    )
    everything.wait_recv()

    mine = outbox[pl.ds(pl.multiple_of(me * rows, rows), rows), :]
    peak = jnp.maximum(jnp.max(inbox[...], axis=0), mine)
    total = jnp.sum(jnp.exp(inbox[...] - peak[None]), axis=0) + jnp.exp(mine - peak)
    total = (peak + jnp.log(total))[:, picks : picks + 1]
    summed = jnp.sum(inbox[...], axis=0) + mine
    logp_ref[...] = summed[:, :picks] - total
    diagonal = lax.broadcasted_iota(jnp.int32, (rows, rows), 0) == lax.broadcasted_iota(jnp.int32, (rows, rows), 1)
    total_ref[...] = jnp.sum(jnp.where(diagonal, total, 0.0), axis=0, keepdims=True)
    everything.wait_send()


def local(hidden_states, head_weight, pick_index, owner_order):
    rows, depth = hidden_states.shape
    width = head_weight.shape[1]
    tokens, picks = pick_index.shape
    chunk_rows = 2 * BLOCKS * rows
    tile_count = -(-width // TILE)
    logp, total = pl.pallas_call(
        kernel,
        out_shape=(
            jax.ShapeDtypeStruct((rows, picks), jnp.float32),
            jax.ShapeDtypeStruct((1, rows), jnp.float32),
        ),
        in_specs=[
            pl.BlockSpec(memory_space=pl.ANY),
            pl.BlockSpec(memory_space=pl.ANY),
            pl.BlockSpec(memory_space=pltpu.VMEM),
            pl.BlockSpec(memory_space=pltpu.VMEM),
        ],
        out_specs=(pl.BlockSpec(memory_space=pltpu.VMEM), pl.BlockSpec(memory_space=pltpu.VMEM)),
        scratch_shapes=[
            pltpu.VMEM((4, chunk_rows, depth), jnp.bfloat16),
            pltpu.VMEM((depth, width), jnp.bfloat16),
            pltpu.VMEM((chunk_rows, width), jnp.float32),
            pltpu.VMEM((chunk_rows, LANES), jnp.float32),
            pltpu.VMEM((chunk_rows, LANES), jnp.float32),
            pltpu.VMEM((chunk_rows, LANES), jnp.float32),
            pltpu.VMEM((tokens, LANES), jnp.int32),
            pltpu.VMEM((tokens, LANES), jnp.int32),
            pltpu.VMEM((tokens, 3 * LANES), jnp.bfloat16),
            pltpu.VMEM((tokens, tokens), jnp.bfloat16),
            pltpu.VMEM((tokens, LANES), jnp.float32),
            pltpu.VMEM((SHARDS - 1, rows, LANES), jnp.float32),
            pltpu.SemaphoreType.DMA,
            pltpu.SemaphoreType.DMA((tile_count,)),
            pltpu.SemaphoreType.DMA((SENDS,)),
            pltpu.SemaphoreType.DMA((len(ARRIVALS),)),
            pltpu.SemaphoreType.DMA((4,)),
            pltpu.SemaphoreType.DMA,
            pltpu.SemaphoreType.DMA,
        ],
        compiler_params=pltpu.CompilerParams(
            collective_id=0, has_side_effects=True, vmem_limit_bytes=62 * 1024 * 1024
        ),
    )(hidden_states, head_weight, pick_index, owner_order.reshape(1, tokens))
    return logp, total.reshape(rows)


def solution(mesh):
    in_specs = (P(("group", "vocab"), None), P(None, "vocab"), P("group", None), P("group"))
    out_specs = (P(("group", "vocab"), None), P(("group", "vocab")))
    return jax.shard_map(local, mesh=mesh, in_specs=in_specs, out_specs=out_specs, check_vma=False)
```

time: 172 us -> 46.5 us (0.27)
  waiting for transfers between devices: 51 us -> 0 us
  other arithmetic: 47.3 us -> 0 us
  Pallas kernels: 0 us -> 41.6 us
  local copies, waits for them, and re-layouts: 28.1 us -> 4.11 us
  matrix products: 16.3 us -> 0 us
  blocking collectives: 14.1 us -> 0 us
  between operations: 14.2 us -> 0.64 us
    all_gather x1 -> x0, waiting for transfers between devices: 50.4 us -> none  [local(): lax.all_gather(hidden_states, 'vocab', axis=0, tiled=True)]
    reduce_sum x19 -> x0, other arithmetic: 45 us -> none  [the longest x16 44 us: select_block(): return jnp.sum(jnp.where(matches, block_logits[:, None, :], 0.0), axis=2)]
    pallas_call x0 -> x1, Pallas kernels: none -> 41.6 us  [local(): pl.pallas_call(kernel, out_shape=(jax.ShapeDtypeStruct((rows, picks), jnp...]
    dot_general x1 -> x0, matrix products: 16.3 us -> none  [local(): jnp.dot(lax.all_gather(hidden_states, 'vocab', axis=0, tiled=True), head_...]
    broadcast_in_dim x17 -> x0, local copies, waits for them, and re-layouts: 16 us -> none  [the longest x16 15.9 us: select_block(): return jnp.sum(jnp.where(matches, block_logits[:, None, :], 0.0), axis=2)]
    all_to_all x1 -> x0, blocking collectives: 14.1 us -> none  [sent_together(): lax.all_to_all(both, axis, split_axis=split_dim, concat_axis=concat_dim,...]
    gather x3 -> x0, local copies, waits for them, and re-layouts: 8.01 us -> none  [the longest x1 3.49 us: local(): jnp.take(local_sum, owner_order, axis=0).reshape(shard_count, own_rows)]
    unnamed x10 -> x3, local copies, waits for them, and re-layouts: 3.35 us -> 4.11 us
  transfers between devices with their start and end apart: 1 -> 0, of which waited for: 1 -> 0; matrix products, arithmetic and copies ran while one was open for 1% -> 0% of each run, Pallas kernels for 0% -> 0%
where the time goes in v1:
time: 46.5 us; the launch traced here: 46.3 us
  Pallas kernels  41.6 us (89%)
  local copies, waits for them, and re-layouts  4.11 us (9%)
  between operations  0.64 us (1%)
    pallas_call x1, Pallas kernels, local(): pl.pallas_call(kernel, out_shape=(jax.ShapeDtypeStruct((rows, picks), jnp...  41.6 us
    unnamed x3, local copies, waits for them, and re-layouts  4.11 us

profile of v1, /device:TPU:1, one launch (start us, length us, event | category | flops | bytes accessed | tf_op | source)
XLA Modules:
  0.0 46.3 jit_solution(10065077528582535129)
XLA Ops:
  0.6 1.7 %copy.6.pick_ref = s32[512,64]{1,0:T(8,128)} copy(s32[512,64]{0,1:T(8,128)} %param.6) | data formatting | bytes 262144 | tf_op args[2]
  2.4 41.6 %shard_map.59 = (f32[16,64]{1,0:T(8,128)}, f32[1,16]{1,0:T(1,128)}) custom-call(bf16[16,4096]{1,0:T(8,128)(2,1)} %x_ref.1, bf16[4096,2432]{1,0:T(8,128)(2,1)} %w_ref.1, s32[512,64]{1,0:T(8,128)} %copy.6.pick_ref, s32[1,512]{1,0:T(1,128)} %bitcast.2), custom_call_target="tpu_custom_call" | custom-call | tf_op jit(solution)/shard_map/pallas_call | solution.py:248
  43.9 1.3 %copy.9 = f32[16,64]{1,0:T(8,128)} copy(f32[16,64]{1,0:T(8,128)} %get-tuple-element.8) | data formatting | bytes 8192
  45.2 1.1 %copy.10 = f32[16]{0:T(128)} copy(f32[16]{0:T(128)} %bitcast.3) | data formatting | bytes 128

commit v2 on v1

--- a/solution.py
+++ b/solution.py
@@ -15,14 +15,18 @@
 BLOCKS = 4
 PLACE = {
     (0, 0): (0, 0), (3, 0): (0, 1), (1, 0): (0, 2), (0, 1): (0, 3),
-    (0, 3): (1, 0), (2, 0): (1, 1), (3, 1): (1, 2), (3, 3): (1, 3),
-    (1, 1): (2, 0), (1, 3): (2, 1), (2, 1): (2, 2), (2, 3): (2, 3),
-    (0, 2): (3, 0), (3, 2): (3, 1), (1, 2): (3, 2), (2, 2): (3, 3),
+    (0, 3): (1, 0), (2, 0): (1, 1), (0, 2): (1, 2), (3, 1): (1, 3),
+    (3, 3): (2, 0), (1, 1): (2, 1), (1, 3): (2, 2), (2, 1): (2, 3),
+    (2, 3): (3, 0), (2, 2): (3, 1), (3, 2): (3, 2), (1, 2): (3, 3),
 }
-HALVED = ((2, 0), (0, 2), (3, 2), (1, 2), (2, 2))
+HALVED = ((3, 2), (1, 2))
 WHOLE = tuple(rel for rel in PLACE if rel not in HALVED and rel != (0, 0))
 ARRIVALS = [(rel, None) for rel in WHOLE] + [(rel, half) for rel in HALVED for half in (0, 1)]
 RECV = {key: number for number, key in enumerate(ARRIVALS)}
+OTHERS = sorted(
+    ((dx, dz, dc) for dx in range(SIDE) for dz in range(SIDE) for dc in range(2) if dx or dz or dc),
+    key=lambda step: -min(step[0], SIDE - step[0]) - min(step[1], SIDE - step[1]),
+)
 SENDS = 40
 
 
@@ -32,12 +36,13 @@
 
 def kernel(
     x_ref, w_ref, pick_ref, order_ref, logp_ref, total_ref,
-    hidden, weight, logits, top, mass, found, low, high, pieces, perm, outbox, inbox,
-    own_sem, weight_sem, send_sem, recv_sem, pair_sem, out_sem, in_sem,
+    hidden, weight, logits, top, mass, found, chosen_ref, low, high, pieces, perm,
+    outbox, inbox, sums_out, sums_in,
+    own_sem, pick_sem, weight_sem, send_sem, recv_sem, pair_sem, out_sem, in_sem, sums_out_sem, sums_in_sem,
 ):
     rows, depth = x_ref.shape
     width = w_ref.shape[1]
-    tokens, picks = pick_ref.shape
+    picks, tokens = pick_ref.shape
     half_depth = depth // 2
     chunk_rows = 2 * BLOCKS * rows
     tiles = [(start, min(TILE, width - start)) for start in range(0, width, TILE)]
@@ -53,6 +58,7 @@
 
     first_up, first_down = at(1, 0, core), at(3, 0, core)
     second_up, second_down = at(0, 1, core), at(0, 3, core)
+    first_far, second_far = at(2, 0, core), at(0, 2, core)
 
     def block(rel, half=None, other=0):
         chunk, slot = PLACE[rel]
@@ -63,6 +69,8 @@
 
     own_copy = pltpu.make_async_copy(x_ref, block((0, 0)), own_sem)
     own_copy.start()
+    pick_copy = pltpu.make_async_copy(pick_ref, chosen_ref, pick_sem)
+    pick_copy.start()
     weight_copies = []
     for number, (start, size) in enumerate(tiles):
         copy = pltpu.make_async_copy(
@@ -72,21 +80,11 @@
         weight_copies.append(copy)
 
     barrier = pltpu.get_barrier_semaphore()
-    for partner in (first_up, first_down, second_up, second_down, pair):
+    for partner in (first_up, first_down, second_up, second_down, first_far, second_far, pair):
         pl.semaphore_signal(barrier, inc=1, device_id={"vocab": partner}, device_id_type=MESH)
 
-    order = jnp.broadcast_to(order_ref[...].astype(jnp.float32), (LANES, tokens))
-    order = jnp.transpose(order)
-    lanes = lax.broadcasted_iota(jnp.int32, (tokens, LANES), 1).astype(jnp.float32)
-    for start in range(0, tokens, LANES):
-        perm[:, pl.ds(start, LANES)] = jnp.where(order == lanes + start, 1.0, 0.0).astype(jnp.bfloat16)
-    places = pick_ref[...] - me * width
-    places = jnp.concatenate([places, places], axis=1)
-    low[...] = places & (LANES - 1)
-    high[...] = places >> 7
-
     own_copy.wait()
-    pl.semaphore_wait(barrier, 5)
+    pl.semaphore_wait(barrier, 7)
 
     started = []
 
@@ -121,15 +119,13 @@
             arrived(rel, 1)
         else:
             arrived(rel)
-        if rel == (3, 0):
-            across(rel, (2, 0), first_up, 0)
-        if rel == (1, 0):
-            across(rel, (2, 0), first_down, 1)
         if rel[1] == 0:
             along_second(rel)
-        if rel[1] == 3:
+        if rel == (2, 0):
+            across(rel, (2, 2), second_far)
+        if rel[0] in (1, 3) and rel[1] == 3:
             across(rel, (rel[0], 2), second_up, 0)
-        if rel[1] == 1:
+        if rel[0] in (1, 3) and rel[1] == 1:
             across(rel, (rel[0], 2), second_down, 1)
         to_pair(rel)
 
@@ -144,13 +140,29 @@
     across((0, 0), (1, 0), first_down)
     along_second((0, 0))
     to_pair((0, 0))
+    across((0, 0), (2, 0), first_far)
+    across((0, 0), (0, 2), second_far)
+
+    order = jnp.broadcast_to(order_ref[...].astype(jnp.float32), (LANES, tokens))
+    order = jnp.transpose(order).reshape(SHARDS, 2, rows // 2, LANES)
+    order = jnp.concatenate([order[:, 0].reshape(-1, LANES), order[:, 1].reshape(-1, LANES)], axis=0)
+    lanes = lax.broadcasted_iota(jnp.int32, (tokens, LANES), 1).astype(jnp.float32)
+    for start in range(0, tokens, LANES):
+        perm[:, pl.ds(start, LANES)] = jnp.where(order == lanes + start, 1.0, 0.0).astype(jnp.bfloat16)
+    pick_copy.wait()
+    for start in range(0, tokens, LANES):
+        places = chosen_ref[:, pl.ds(start, LANES)] - me * width
+        places = jnp.transpose(jnp.concatenate([places, places], axis=0))
+        low[pl.ds(start, LANES), :] = places & (LANES - 1)
+        high[pl.ds(start, LANES), :] = places >> 7
+
     for rel in ((3, 0), (1, 0), (0, 1), (0, 3)):
         service(rel)
 
     services = {
-        (0, 1): ((2, 0),), (0, 3): ((3, 3), (3, 1)),
+        (0, 2): ((2, 0), (0, 2)), (0, 4): ((3, 1), (3, 3)),
         (1, 1): ((1, 1), (1, 3)), (1, 3): ((2, 1), (2, 3)),
-        (2, 1): ((0, 2), (3, 2)), (2, 3): ((1, 2), (2, 2)),
+        (2, 2): ((2, 2),), (2, 4): ((3, 2), (1, 2)),
     }
 
     def positions(chunk):
@@ -211,32 +223,54 @@
         for k, spot in enumerate(spots):
             pieces[pl.ds(spot, rows), :] = parts[k * rows : (k + 1) * rows]
 
-    sorted_parts = jnp.dot(perm[...], pieces[...], preferred_element_type=jnp.float32)
-    outbox[...] = (sorted_parts[:, :LANES] + sorted_parts[:, LANES : 2 * LANES]) + sorted_parts[:, 2 * LANES :]
-
-    for step in range(1, SHARDS):
-        owner = (me + step) % SHARDS
-        pltpu.make_async_remote_copy(
-            src_ref=outbox.at[pl.ds(pl.multiple_of(owner * rows, rows), rows), :], dst_ref=inbox.at[step - 1],
-            send_sem=out_sem, recv_sem=in_sem, device_id={"vocab": owner}, device_id_type=MESH,
-        ).start()
+    parts = jnp.dot(perm[...], pieces[...], preferred_element_type=jnp.float32)
+    ordered = (parts[:, :LANES] + parts[:, LANES : 2 * LANES]) + parts[:, 2 * LANES :]
+    upper, lower = ordered[: tokens // 2], ordered[tokens // 2 :]
+    lane = lax.broadcasted_iota(jnp.int32, upper.shape, 1)
+    outbox[...] = jnp.where(lane < picks, upper, pltpu.roll(lower, picks, 1)).reshape(outbox.shape)
+    step = lax.broadcasted_iota(jnp.int32, upper.shape, 0) % (rows // 2)
+    sums = jnp.where(lane == picks + step, upper, 0.0) + jnp.where(lane == picks + rows // 2 + step, lower, 0.0)
+    for shard in range(SHARDS):
+        part = sums[shard * (rows // 2) : (shard + 1) * (rows // 2)]
+        sums_out[shard] = jnp.sum(part, axis=0, keepdims=True)
+
+    for number, (dx, dz, dc) in enumerate(OTHERS):
+        owner = flat(x + dx, z + dz, (core + dc) % 2)
+        for source, target, sends, receives in (
+            (outbox, inbox, out_sem, in_sem), (sums_out, sums_in, sums_out_sem, sums_in_sem)
+        ):
+            pltpu.make_async_remote_copy(
+                src_ref=source.at[owner], dst_ref=target.at[number], send_sem=sends, recv_sem=receives,
+                device_id={"vocab": owner}, device_id_type=MESH,
+            ).start()
     for copy in started:
         copy.wait_send()
-    everything = pltpu.make_async_remote_copy(
-        src_ref=inbox, dst_ref=inbox, send_sem=out_sem, recv_sem=in_sem,
-        device_id={"vocab": pair}, device_id_type=MESH,
-    )
-    everything.wait_recv()
-
-    mine = outbox[pl.ds(pl.multiple_of(me * rows, rows), rows), :]
-    peak = jnp.maximum(jnp.max(inbox[...], axis=0), mine)
-    total = jnp.sum(jnp.exp(inbox[...] - peak[None]), axis=0) + jnp.exp(mine - peak)
-    total = (peak + jnp.log(total))[:, picks : picks + 1]
-    summed = jnp.sum(inbox[...], axis=0) + mine
-    logp_ref[...] = summed[:, :picks] - total
-    diagonal = lax.broadcasted_iota(jnp.int32, (rows, rows), 0) == lax.broadcasted_iota(jnp.int32, (rows, rows), 1)
-    total_ref[...] = jnp.sum(jnp.where(diagonal, total, 0.0), axis=0, keepdims=True)
-    everything.wait_send()
+
+    def exchanged(target, sends, receives):
+        return pltpu.make_async_remote_copy(
+            src_ref=target, dst_ref=target, send_sem=sends, recv_sem=receives,
+            device_id={"vocab": pair}, device_id_type=MESH,
+        )
+
+    picks_moved = exchanged(inbox, out_sem, in_sem)
+    sums_moved = exchanged(sums_in, sums_out_sem, sums_in_sem)
+    sums_moved.wait_recv()
+    own_sum = sums_out[me]
+    peak = jnp.maximum(jnp.max(sums_in[...], axis=0), own_sum)
+    total = jnp.sum(jnp.exp(sums_in[...] - peak[None]), axis=0) + jnp.exp(own_sum - peak)
+    total = peak + jnp.log(total)
+    total_ref[...] = total[:, picks : picks + rows]
+    lane = lax.broadcasted_iota(jnp.int32, (rows // 2, LANES), 1)
+    step = lax.broadcasted_iota(jnp.int32, (rows // 2, LANES), 0)
+    spread = jnp.broadcast_to(total, (rows // 2, LANES))
+    first = jnp.sum(jnp.where(lane == picks + step, spread, 0.0), axis=1, keepdims=True)
+    second = jnp.sum(jnp.where(lane == picks + rows // 2 + step, spread, 0.0), axis=1, keepdims=True)
+    picks_moved.wait_recv()
+    summed = jnp.sum(inbox[...], axis=0) + outbox[me] - jnp.where(lane < picks, first, second)
+    logp_ref[pl.ds(0, rows // 2), :] = summed[:, :picks]
+    logp_ref[pl.ds(rows // 2, rows // 2), :] = pltpu.roll(summed, picks, 1)[:, :picks]
+    sums_moved.wait_send()
+    picks_moved.wait_send()
 
 
 def local(hidden_states, head_weight, pick_index, owner_order):
@@ -254,7 +288,7 @@
         in_specs=[
             pl.BlockSpec(memory_space=pl.ANY),
             pl.BlockSpec(memory_space=pl.ANY),
-            pl.BlockSpec(memory_space=pltpu.VMEM),
+            pl.BlockSpec(memory_space=pl.ANY),
             pl.BlockSpec(memory_space=pltpu.VMEM),
         ],
         out_specs=(pl.BlockSpec(memory_space=pltpu.VMEM), pl.BlockSpec(memory_space=pltpu.VMEM)),
@@ -265,12 +299,16 @@
             pltpu.VMEM((chunk_rows, LANES), jnp.float32),
             pltpu.VMEM((chunk_rows, LANES), jnp.float32),
             pltpu.VMEM((chunk_rows, LANES), jnp.float32),
+            pltpu.VMEM((picks, tokens), jnp.int32),
             pltpu.VMEM((tokens, LANES), jnp.int32),
             pltpu.VMEM((tokens, LANES), jnp.int32),
             pltpu.VMEM((tokens, 3 * LANES), jnp.bfloat16),
             pltpu.VMEM((tokens, tokens), jnp.bfloat16),
-            pltpu.VMEM((tokens, LANES), jnp.float32),
-            pltpu.VMEM((SHARDS - 1, rows, LANES), jnp.float32),
+            pltpu.VMEM((SHARDS, rows // 2, LANES), jnp.float32),
+            pltpu.VMEM((SHARDS - 1, rows // 2, LANES), jnp.float32),
+            pltpu.VMEM((SHARDS, 1, LANES), jnp.float32),
+            pltpu.VMEM((SHARDS - 1, 1, LANES), jnp.float32),
+            pltpu.SemaphoreType.DMA,
             pltpu.SemaphoreType.DMA,
             pltpu.SemaphoreType.DMA((tile_count,)),
             pltpu.SemaphoreType.DMA((SENDS,)),
@@ -278,11 +316,13 @@
             pltpu.SemaphoreType.DMA((4,)),
             pltpu.SemaphoreType.DMA,
             pltpu.SemaphoreType.DMA,
+            pltpu.SemaphoreType.DMA,
+            pltpu.SemaphoreType.DMA,
         ],
         compiler_params=pltpu.CompilerParams(
             collective_id=0, has_side_effects=True, vmem_limit_bytes=62 * 1024 * 1024
         ),
-    )(hidden_states, head_weight, pick_index, owner_order.reshape(1, tokens))
+    )(hidden_states, head_weight, pick_index.T, owner_order.reshape(1, tokens))
     return logp, total.reshape(rows)
 
 

time: 46.5 us -> 46.1 us (level)
  local copies, waits for them, and re-layouts: 4.11 us -> 2.43 us
  Pallas kernels: 41.6 us -> 42.8 us
    unnamed x3 -> x2, local copies, waits for them, and re-layouts: 4.11 us -> 2.43 us
    pallas_call x1, Pallas kernels: 41.6 us -> 42.8 us  [local(): pl.pallas_call(kernel, out_shape=(jax.ShapeDtypeStruct((rows, picks), jnp...]
where the time goes in v2:
time: 46.1 us; the launch traced here: 45.9 us
  Pallas kernels  42.8 us (93%)
  local copies, waits for them, and re-layouts  2.43 us (5%)
  between operations  0.64 us (1%)
    pallas_call x1, Pallas kernels, local(): pl.pallas_call(kernel, out_shape=(jax.ShapeDtypeStruct((rows, picks), jnp...  42.8 us
    unnamed x2, local copies, waits for them, and re-layouts  2.43 us

profile of v2, /device:TPU:1, one launch (start us, length us, event | category | flops | bytes accessed | tf_op | source)
XLA Modules:
  0.0 45.9 jit_solution(11325496720913616049)
XLA Ops:
  0.6 42.8 %shard_map.59 = (f32[16,64]{1,0:T(8,128)}, f32[1,16]{1,0:T(1,128)}) custom-call(bf16[16,4096]{1,0:T(8,128)(2,1)} %x_ref.1, bf16[4096,2432]{1,0:T(8,128)(2,1)} %w_ref.1, s32[64,512]{1,0:T(8,128)} %bitcast.3, s32[1,512]{1,0:T(1,128)} %bitcast.4), custom_call_target="tpu_custom_call" | custom-call | tf_op jit(solution)/shard_map/pallas_call | solution.py:282
  43.4 1.3 %copy.8 = f32[16,64]{1,0:T(8,128)} copy(f32[16,64]{1,0:T(8,128)} %get-tuple-element.8) | data formatting | bytes 8192
  44.7 1.1 %copy.9 = f32[16]{0:T(128)} copy(f32[16]{0:T(128)} %bitcast.5) | data formatting | bytes 128

commit v3 on v2

--- a/solution.py
+++ b/solution.py
@@ -19,15 +19,17 @@
     (3, 3): (2, 0), (1, 1): (2, 1), (1, 3): (2, 2), (2, 1): (2, 3),
     (2, 3): (3, 0), (2, 2): (3, 1), (3, 2): (3, 2), (1, 2): (3, 3),
 }
-HALVED = ((3, 2), (1, 2))
-WHOLE = tuple(rel for rel in PLACE if rel not in HALVED and rel != (0, 0))
-ARRIVALS = [(rel, None) for rel in WHOLE] + [(rel, half) for rel in HALVED for half in (0, 1)]
-RECV = {key: number for number, key in enumerate(ARRIVALS)}
+PIECES = {rel: 1 for rel in PLACE if rel != (0, 0)}
+PIECES.update({rel: 2 for rel in ((3, 0), (1, 0), (3, 1), (3, 3), (1, 1), (1, 3), (2, 0), (0, 2), (3, 2), (1, 2), (2, 2))})
+RECV = {}
+for rel, count in PIECES.items():
+    for piece in range(count):
+        RECV[rel, piece] = len(RECV)
 OTHERS = sorted(
     ((dx, dz, dc) for dx in range(SIDE) for dz in range(SIDE) for dc in range(2) if dx or dz or dc),
     key=lambda step: -min(step[0], SIDE - step[0]) - min(step[1], SIDE - step[1]),
 )
-SENDS = 40
+SENDS = 80
 
 
 def flat(x, z, core):
@@ -36,14 +38,13 @@
 
 def kernel(
     x_ref, w_ref, pick_ref, order_ref, logp_ref, total_ref,
-    hidden, weight, logits, top, mass, found, chosen_ref, low, high, pieces, perm,
+    hidden, weight, logits, top, mass, found, chosen_ref, order_row, low, high, pieces, perm,
     outbox, inbox, sums_out, sums_in,
-    own_sem, pick_sem, weight_sem, send_sem, recv_sem, pair_sem, out_sem, in_sem, sums_out_sem, sums_in_sem,
+    own_sem, pick_sem, order_sem, weight_sem, send_sem, recv_sem, pair_sem, out_sem, in_sem, sums_out_sem, sums_in_sem,
 ):
     rows, depth = x_ref.shape
     width = w_ref.shape[1]
     picks, tokens = pick_ref.shape
-    half_depth = depth // 2
     chunk_rows = 2 * BLOCKS * rows
     tiles = [(start, min(TILE, width - start)) for start in range(0, width, TILE)]
 
@@ -58,33 +59,32 @@
 
     first_up, first_down = at(1, 0, core), at(3, 0, core)
     second_up, second_down = at(0, 1, core), at(0, 3, core)
-    first_far, second_far = at(2, 0, core), at(0, 2, core)
-
-    def block(rel, half=None, other=0):
+
+    def block(rel, piece=0, pieces=1, other=0):
         chunk, slot = PLACE[rel]
-        row = (slot + BLOCKS * other) * rows
-        if half is None:
-            return hidden.at[chunk, pl.ds(row, rows), :]
-        return hidden.at[chunk, pl.ds(row, rows), pl.ds(half * half_depth, half_depth)]
+        size = depth // pieces
+        return hidden.at[chunk, pl.ds((slot + BLOCKS * other) * rows, rows), pl.ds(piece * size, size)]
 
     own_copy = pltpu.make_async_copy(x_ref, block((0, 0)), own_sem)
     own_copy.start()
     pick_copy = pltpu.make_async_copy(pick_ref, chosen_ref, pick_sem)
     pick_copy.start()
+    order_copy = pltpu.make_async_copy(order_ref, order_row, order_sem)
+    order_copy.start()
     weight_copies = []
     for number, (start, size) in enumerate(tiles):
         copy = pltpu.make_async_copy(
             w_ref.at[:, pl.ds(start, size)], weight.at[:, pl.ds(start, size)], weight_sem.at[number]
         )
-        copy.start()
+        copy.start(priority=1)
         weight_copies.append(copy)
 
     barrier = pltpu.get_barrier_semaphore()
-    for partner in (first_up, first_down, second_up, second_down, first_far, second_far, pair):
+    for partner in (first_up, first_down, second_up, second_down, pair):
         pl.semaphore_signal(barrier, inc=1, device_id={"vocab": partner}, device_id_type=MESH)
 
     own_copy.wait()
-    pl.semaphore_wait(barrier, 7)
+    pl.semaphore_wait(barrier, 5)
 
     started = []
 
@@ -96,54 +96,49 @@
         copy.start()
         started.append(copy)
 
-    def arrived(rel, half=None):
-        ref = block(rel, half)
+    def wait_for(ref, sem):
         pltpu.make_async_remote_copy(
-            src_ref=ref, dst_ref=ref, send_sem=send_sem.at[0], recv_sem=recv_sem.at[RECV[rel, half]],
+            src_ref=ref, dst_ref=ref, send_sem=send_sem.at[0], recv_sem=sem,
             device_id={"vocab": pair}, device_id_type=MESH,
         ).wait_recv()
 
-    def across(rel, to_rel, to, half=None):
-        push(block(rel, half), block(to_rel, half), recv_sem.at[RECV[to_rel, half]], to)
+    def arrived(rel, *pieces):
+        for piece in pieces or range(PIECES[rel]):
+            wait_for(block(rel, piece, PIECES[rel]), recv_sem.at[RECV[rel, piece]])
+
+    def across(rel, to_rel, to, piece=0):
+        count = PIECES[to_rel]
+        push(block(rel, piece, count), block(to_rel, piece, count), recv_sem.at[RECV[to_rel, piece]], to)
+
+    def along_second(rel, piece=0):
+        across(rel, (rel[0], 3), second_up, piece)
+        across(rel, (rel[0], 1), second_down, piece)
 
     def to_pair(rel):
         push(block(rel), block(rel, other=1), pair_sem.at[PLACE[rel][0]], pair)
 
-    def along_second(rel):
-        across(rel, (rel[0], 3), second_up)
-        across(rel, (rel[0], 1), second_down)
-
     def service(rel):
-        if rel in HALVED:
-            arrived(rel, 0)
-            arrived(rel, 1)
-        else:
-            arrived(rel)
-        if rel[1] == 0:
+        arrived(rel)
+        if rel == (2, 0):
             along_second(rel)
-        if rel == (2, 0):
-            across(rel, (2, 2), second_far)
-        if rel[0] in (1, 3) and rel[1] == 3:
+        elif rel[1] == 3:
             across(rel, (rel[0], 2), second_up, 0)
-        if rel[0] in (1, 3) and rel[1] == 1:
+        elif rel[1] == 1:
             across(rel, (rel[0], 2), second_down, 1)
         to_pair(rel)
 
     def pair_arrived(chunk):
-        ref = hidden.at[chunk, pl.ds(BLOCKS * rows, BLOCKS * rows), :]
-        pltpu.make_async_remote_copy(
-            src_ref=ref, dst_ref=ref, send_sem=send_sem.at[0], recv_sem=pair_sem.at[chunk],
-            device_id={"vocab": pair}, device_id_type=MESH,
-        ).wait_recv()
-
-    across((0, 0), (3, 0), first_up)
-    across((0, 0), (1, 0), first_down)
+        wait_for(hidden.at[chunk, pl.ds(BLOCKS * rows, BLOCKS * rows), :], pair_sem.at[chunk])
+
+    across((0, 0), (3, 0), first_up, 0)
+    across((0, 0), (1, 0), first_down, 1)
     along_second((0, 0))
+    across((0, 0), (3, 0), first_up, 1)
+    across((0, 0), (1, 0), first_down, 0)
     to_pair((0, 0))
-    across((0, 0), (2, 0), first_far)
-    across((0, 0), (0, 2), second_far)
-
-    order = jnp.broadcast_to(order_ref[...].astype(jnp.float32), (LANES, tokens))
+
+    order_copy.wait()
+    order = jnp.broadcast_to(order_row[...].astype(jnp.float32), (LANES, tokens))
     order = jnp.transpose(order).reshape(SHARDS, 2, rows // 2, LANES)
     order = jnp.concatenate([order[:, 0].reshape(-1, LANES), order[:, 1].reshape(-1, LANES)], axis=0)
     lanes = lax.broadcasted_iota(jnp.int32, (tokens, LANES), 1).astype(jnp.float32)
@@ -156,13 +151,20 @@
         low[pl.ds(start, LANES), :] = places & (LANES - 1)
         high[pl.ds(start, LANES), :] = places >> 7
 
-    for rel in ((3, 0), (1, 0), (0, 1), (0, 3)):
-        service(rel)
+    for turn in (0, 1):
+        for rel, half, on in (((3, 0), turn, first_up), ((1, 0), 1 - turn, first_down)):
+            arrived(rel, half)
+            if turn == 0:
+                across(rel, (2, 0), on, half)
+            along_second(rel, half)
+            if turn == 1:
+                to_pair(rel)
+    service((0, 1))
+    service((0, 3))
 
     services = {
-        (0, 2): ((2, 0), (0, 2)), (0, 4): ((3, 1), (3, 3)),
-        (1, 1): ((1, 1), (1, 3)), (1, 3): ((2, 1), (2, 3)),
-        (2, 2): ((2, 2),), (2, 4): ((3, 2), (1, 2)),
+        (0, 2): ((2, 0),), (0, 4): ((0, 2), (3, 3), (3, 1), (1, 1), (1, 3)),
+        (1, 1): ((2, 1), (2, 3)), (2, 2): ((2, 2), (3, 2), (1, 2)),
     }
 
     def positions(chunk):
@@ -196,26 +198,14 @@
         mass[...] = total
         found[...] = chosen
 
-    for chunk in range(4):
-        pair_arrived(chunk)
-        spots = positions(chunk)
-        for number, (start, size) in enumerate(tiles):
-            if chunk == 0:
-                weight_copies[number].wait()
-            logits[:, pl.ds(start, size)] = jnp.dot(
-                hidden[chunk], weight[:, pl.ds(start, size)], preferred_element_type=jnp.float32
-            )
-            if number > 0:
-                digest(chunk, number - 1, spots)
-            for rel in services.get((chunk, number), ()):
-                service(rel)
+    def finish(chunk, spots):
         digest(chunk, len(tiles) - 1, spots)
         peak = jnp.max(top[...], axis=1, keepdims=True)
         lse = peak + jnp.log(jnp.sum(mass[...] * jnp.exp(top[...] - peak), axis=1, keepdims=True))
         lane = lax.broadcasted_iota(jnp.int32, (chunk_rows, LANES), 1)
         rest = jnp.where(lane < picks, found[...], lse)
         parts = []
-        for _ in range(3):
+        for _ in range(2):
             part = rest.astype(jnp.bfloat16)
             rest = rest - part.astype(jnp.float32)
             parts.append(part)
@@ -223,8 +213,25 @@
         for k, spot in enumerate(spots):
             pieces[pl.ds(spot, rows), :] = parts[k * rows : (k + 1) * rows]
 
+    for chunk in range(4):
+        pair_arrived(chunk)
+        if chunk == 0:
+            for copy in weight_copies:
+                copy.wait()
+        for number, (start, size) in enumerate(tiles):
+            logits[:, pl.ds(start, size)] = jnp.dot(
+                hidden[chunk], weight[:, pl.ds(start, size)], preferred_element_type=jnp.float32
+            )
+            if number > 0:
+                digest(chunk, number - 1, positions(chunk))
+            elif chunk > 0:
+                finish(chunk - 1, positions(chunk - 1))
+            for rel in services.get((chunk, number), ()):
+                service(rel)
+    finish(3, positions(3))
+
     parts = jnp.dot(perm[...], pieces[...], preferred_element_type=jnp.float32)
-    ordered = (parts[:, :LANES] + parts[:, LANES : 2 * LANES]) + parts[:, 2 * LANES :]
+    ordered = parts[:, :LANES] + parts[:, LANES:]
     upper, lower = ordered[: tokens // 2], ordered[tokens // 2 :]
     lane = lax.broadcasted_iota(jnp.int32, upper.shape, 1)
     outbox[...] = jnp.where(lane < picks, upper, pltpu.roll(lower, picks, 1)).reshape(outbox.shape)
@@ -279,6 +286,7 @@
     tokens, picks = pick_index.shape
     chunk_rows = 2 * BLOCKS * rows
     tile_count = -(-width // TILE)
+    operands = (hidden_states, head_weight, pick_index.T, owner_order.reshape(1, tokens))
     logp, total = pl.pallas_call(
         kernel,
         out_shape=(
@@ -286,10 +294,10 @@
             jax.ShapeDtypeStruct((1, rows), jnp.float32),
         ),
         in_specs=[
-            pl.BlockSpec(memory_space=pl.ANY),
-            pl.BlockSpec(memory_space=pl.ANY),
-            pl.BlockSpec(memory_space=pl.ANY),
-            pl.BlockSpec(memory_space=pltpu.VMEM),
+            pl.BlockSpec(memory_space=pltpu.HBM),
+            pl.BlockSpec(memory_space=pltpu.HBM),
+            pl.BlockSpec(memory_space=pltpu.HBM),
+            pl.BlockSpec(memory_space=pltpu.HBM),
         ],
         out_specs=(pl.BlockSpec(memory_space=pltpu.VMEM), pl.BlockSpec(memory_space=pltpu.VMEM)),
         scratch_shapes=[
@@ -300,9 +308,10 @@
             pltpu.VMEM((chunk_rows, LANES), jnp.float32),
             pltpu.VMEM((chunk_rows, LANES), jnp.float32),
             pltpu.VMEM((picks, tokens), jnp.int32),
+            pltpu.VMEM((1, tokens), jnp.int32),
             pltpu.VMEM((tokens, LANES), jnp.int32),
             pltpu.VMEM((tokens, LANES), jnp.int32),
-            pltpu.VMEM((tokens, 3 * LANES), jnp.bfloat16),
+            pltpu.VMEM((tokens, 2 * LANES), jnp.bfloat16),
             pltpu.VMEM((tokens, tokens), jnp.bfloat16),
             pltpu.VMEM((SHARDS, rows // 2, LANES), jnp.float32),
             pltpu.VMEM((SHARDS - 1, rows // 2, LANES), jnp.float32),
@@ -310,9 +319,10 @@
             pltpu.VMEM((SHARDS - 1, 1, LANES), jnp.float32),
             pltpu.SemaphoreType.DMA,
             pltpu.SemaphoreType.DMA,
+            pltpu.SemaphoreType.DMA,
             pltpu.SemaphoreType.DMA((tile_count,)),
             pltpu.SemaphoreType.DMA((SENDS,)),
-            pltpu.SemaphoreType.DMA((len(ARRIVALS),)),
+            pltpu.SemaphoreType.DMA((len(RECV),)),
             pltpu.SemaphoreType.DMA((4,)),
             pltpu.SemaphoreType.DMA,
             pltpu.SemaphoreType.DMA,
@@ -320,9 +330,9 @@
             pltpu.SemaphoreType.DMA,
         ],
         compiler_params=pltpu.CompilerParams(
-            collective_id=0, has_side_effects=True, vmem_limit_bytes=62 * 1024 * 1024
+            collective_id=0, has_side_effects=True, vmem_limit_bytes=48 * 1024 * 1024
         ),
-    )(hidden_states, head_weight, pick_index.T, owner_order.reshape(1, tokens))
+    )(*(pltpu.with_memory_space_constraint(a, pltpu.HBM) for a in operands))
     return logp, total.reshape(rows)
 
 

time: 46.1 us -> 36.4 us (0.79)
  Pallas kernels: 42.8 us -> 34.6 us
  local copies, waits for them, and re-layouts: 2.43 us -> 1.11 us
    pallas_call x1, Pallas kernels: 42.8 us -> 34.6 us  [local(): pl.pallas_call(kernel, out_shape=(jax.ShapeDtypeStruct((rows, picks), jnp...]
    unnamed x2, local copies, waits for them, and re-layouts: 2.43 us -> 1.11 us
where the time goes in v3:
time: 36.4 us; the launch traced here: 36.3 us
  Pallas kernels  34.6 us (95%)
  local copies, waits for them, and re-layouts  1.11 us (3%)
  between operations  0.64 us (2%)
    pallas_call x1, Pallas kernels, local(): pl.pallas_call(kernel, out_shape=(jax.ShapeDtypeStruct((rows, picks), jnp...  34.6 us
    unnamed x2, local copies, waits for them, and re-layouts  1.11 us

profile of v3, /device:TPU:1, one launch (start us, length us, event | category | flops | bytes accessed | tf_op | source)
XLA Modules:
  0.0 36.3 jit_solution(926368570571747975)
XLA Ops:
  0.6 34.6 %shard_map.59 = (f32[16,64]{1,0:T(8,128)S(1)}, f32[1,16]{1,0:T(1,128)S(1)}) custom-call(bf16[16,4096]{1,0:T(8,128)(2,1)} %x_ref.1, bf16[4096,2432]{1,0:T(8,128)(2,1)} %w_ref.1, s32[64,512]{1,0:T(8,128)} %bitcast.4, s32[1,512]{1,0:T(1,128)} %bitcast.5), custom_call_target="tpu_custom_call" | custom-call | tf_op jit(solution)/shard_map/pallas_call | solution.py:290
  35.2 0.6 %copy.8 = f32[16,64]{1,0:T(8,128)} copy(f32[16,64]{1,0:T(8,128)S(1)} %get-tuple-element.8) | data formatting | bytes 8192
  35.8 0.5 %copy.9 = f32[16]{0:T(128)} copy(f32[16]{0:T(128)S(1)} %bitcast.3) | data formatting | bytes 128

commit v4 on v3

--- a/solution.py
+++ b/solution.py
@@ -12,12 +12,22 @@
 SHARDS = 2 * SIDE * SIDE
 LANES = 128
 TILE = 512
-BLOCKS = 4
-PLACE = {
-    (0, 0): (0, 0), (3, 0): (0, 1), (1, 0): (0, 2), (0, 1): (0, 3),
-    (0, 3): (1, 0), (2, 0): (1, 1), (0, 2): (1, 2), (3, 1): (1, 3),
-    (3, 3): (2, 0), (1, 1): (2, 1), (1, 3): (2, 2), (2, 1): (2, 3),
-    (2, 3): (3, 0), (2, 2): (3, 1), (3, 2): (3, 2), (1, 2): (3, 3),
+OWN = (
+    ((0, 0), (3, 0), (1, 0), (0, 1), (0, 3)),
+    ((2, 0), (3, 3), (3, 1), (1, 1)),
+    ((1, 3), (2, 1), (2, 3), (0, 2)),
+    ((2, 2), (3, 2), (1, 2)),
+)
+HANDED = (
+    ((0, 0), (3, 0), (1, 0)),
+    ((0, 1), (0, 3), (2, 0), (3, 3)),
+    ((3, 1), (1, 1), (1, 3), (2, 1)),
+    ((2, 3), (0, 2), (2, 2), (3, 2), (1, 2)),
+)
+COUNTS = tuple(len(own) + len(handed) for own, handed in zip(OWN, HANDED))
+PLACE = {rel: (chunk, slot) for chunk, rels in enumerate(OWN) for slot, rel in enumerate(rels)}
+PLACE_HANDED = {
+    rel: (chunk, len(OWN[chunk]) + slot) for chunk, rels in enumerate(HANDED) for slot, rel in enumerate(rels)
 }
 PIECES = {rel: 1 for rel in PLACE if rel != (0, 0)}
 PIECES.update({rel: 2 for rel in ((3, 0), (1, 0), (3, 1), (3, 3), (1, 1), (1, 3), (2, 0), (0, 2), (3, 2), (1, 2), (2, 2))})
@@ -45,7 +55,6 @@
     rows, depth = x_ref.shape
     width = w_ref.shape[1]
     picks, tokens = pick_ref.shape
-    chunk_rows = 2 * BLOCKS * rows
     tiles = [(start, min(TILE, width - start)) for start in range(0, width, TILE)]
 
     me = lax.axis_index("vocab")
@@ -61,9 +70,9 @@
     second_up, second_down = at(0, 1, core), at(0, 3, core)
 
     def block(rel, piece=0, pieces=1, other=0):
-        chunk, slot = PLACE[rel]
+        chunk, slot = (PLACE_HANDED if other else PLACE)[rel]
         size = depth // pieces
-        return hidden.at[chunk, pl.ds((slot + BLOCKS * other) * rows, rows), pl.ds(piece * size, size)]
+        return hidden.at[chunk, pl.ds(slot * rows, rows), pl.ds(piece * size, size)]
 
     own_copy = pltpu.make_async_copy(x_ref, block((0, 0)), own_sem)
     own_copy.start()
@@ -114,8 +123,8 @@
         across(rel, (rel[0], 3), second_up, piece)
         across(rel, (rel[0], 1), second_down, piece)
 
-    def to_pair(rel):
-        push(block(rel), block(rel, other=1), pair_sem.at[PLACE[rel][0]], pair)
+    def to_pair(rel, piece=0, count=1):
+        push(block(rel, piece, count), block(rel, piece, count, 1), pair_sem.at[PLACE_HANDED[rel][0]], pair)
 
     def service(rel):
         arrived(rel)
@@ -128,7 +137,8 @@
         to_pair(rel)
 
     def pair_arrived(chunk):
-        wait_for(hidden.at[chunk, pl.ds(BLOCKS * rows, BLOCKS * rows), :], pair_sem.at[chunk])
+        handed = pl.ds(len(OWN[chunk]) * rows, len(HANDED[chunk]) * rows)
+        wait_for(hidden.at[chunk, handed, :], pair_sem.at[chunk])
 
     across((0, 0), (3, 0), first_up, 0)
     across((0, 0), (1, 0), first_down, 1)
@@ -156,54 +166,52 @@
             arrived(rel, half)
             if turn == 0:
                 across(rel, (2, 0), on, half)
+            to_pair(rel, half, 2)
             along_second(rel, half)
-            if turn == 1:
-                to_pair(rel)
     service((0, 1))
     service((0, 3))
 
     services = {
-        (0, 2): ((2, 0),), (0, 4): ((0, 2), (3, 3), (3, 1), (1, 1), (1, 3)),
-        (1, 1): ((2, 1), (2, 3)), (2, 2): ((2, 2), (3, 2), (1, 2)),
+        (0, 2): ((2, 0),), (0, 3): ((3, 3), (3, 1)), (0, 4): ((1, 1), (1, 3)),
+        (1, 1): ((0, 2), (2, 1), (2, 3)), (2, 1): ((3, 2), (1, 2)), (2, 2): ((2, 2),),
     }
 
     def positions(chunk):
-        spots = [None] * (2 * BLOCKS)
-        for rel, (number, slot) in PLACE.items():
-            if number == chunk:
-                spots[slot] = at(*rel, core)
-                spots[slot + BLOCKS] = at(*rel, 1 - core)
+        spots = [at(*rel, core) for rel in OWN[chunk]] + [at(*rel, 1 - core) for rel in HANDED[chunk]]
         return [pl.multiple_of(spot * rows, rows) for spot in spots]
 
     def digest(chunk, number, spots):
         start, size = tiles[number]
         first = start // LANES
-        values = [logits[:, pl.ds(start + LANES * k, LANES)] for k in range(size // LANES)]
+        part = pl.ds(0, COUNTS[chunk] * rows)
+        values = [logits[part, pl.ds(start + LANES * k, LANES)] for k in range(size // LANES)]
         best = functools.reduce(jnp.maximum, values)
         if number == 0:
             total = jnp.zeros_like(best)
             chosen = jnp.zeros_like(best)
         else:
-            old = top[...]
+            old = top[part, :]
             best = jnp.maximum(best, old)
-            total = mass[...] * jnp.exp(old - best)
-            chosen = found[...]
+            total = mass[part, :] * jnp.exp(old - best)
+            chosen = found[part, :]
         lane = jnp.concatenate([low[pl.ds(spot, rows), :] for spot in spots], axis=0)
         tile = jnp.concatenate([high[pl.ds(spot, rows), :] for spot in spots], axis=0)
         for k, value in enumerate(values):
             total = total + jnp.exp(value - best)
             taken = jnp.take_along_axis(value, lane, axis=1, mode="promise_in_bounds")
             chosen = jnp.where(tile == first + k, taken, chosen)
-        top[...] = best
-        mass[...] = total
-        found[...] = chosen
+        top[part, :] = best
+        mass[part, :] = total
+        found[part, :] = chosen
 
     def finish(chunk, spots):
         digest(chunk, len(tiles) - 1, spots)
-        peak = jnp.max(top[...], axis=1, keepdims=True)
-        lse = peak + jnp.log(jnp.sum(mass[...] * jnp.exp(top[...] - peak), axis=1, keepdims=True))
-        lane = lax.broadcasted_iota(jnp.int32, (chunk_rows, LANES), 1)
-        rest = jnp.where(lane < picks, found[...], lse)
+        part = pl.ds(0, COUNTS[chunk] * rows)
+        best = top[part, :]
+        peak = jnp.max(best, axis=1, keepdims=True)
+        lse = peak + jnp.log(jnp.sum(mass[part, :] * jnp.exp(best - peak), axis=1, keepdims=True))
+        lane = lax.broadcasted_iota(jnp.int32, best.shape, 1)
+        rest = jnp.where(lane < picks, found[part, :], lse)
         parts = []
         for _ in range(2):
             part = rest.astype(jnp.bfloat16)
@@ -219,8 +227,9 @@
             for copy in weight_copies:
                 copy.wait()
         for number, (start, size) in enumerate(tiles):
-            logits[:, pl.ds(start, size)] = jnp.dot(
-                hidden[chunk], weight[:, pl.ds(start, size)], preferred_element_type=jnp.float32
+            part = pl.ds(0, COUNTS[chunk] * rows)
+            logits[part, pl.ds(start, size)] = jnp.dot(
+                hidden[chunk, part, :], weight[:, pl.ds(start, size)], preferred_element_type=jnp.float32
             )
             if number > 0:
                 digest(chunk, number - 1, positions(chunk))
@@ -284,7 +293,7 @@
     rows, depth = hidden_states.shape
     width = head_weight.shape[1]
     tokens, picks = pick_index.shape
-    chunk_rows = 2 * BLOCKS * rows
+    chunk_rows = max(COUNTS) * rows
     tile_count = -(-width // TILE)
     operands = (hidden_states, head_weight, pick_index.T, owner_order.reshape(1, tokens))
     logp, total = pl.pallas_call(

time: 36.4 us -> 36.4 us (level)
  no operation moved by 1% of the time
where the time goes in v4:
time: 36.4 us; the launch traced here: 36.3 us
  Pallas kernels  34.5 us (95%)
  local copies, waits for them, and re-layouts  1.11 us (3%)
  between operations  0.64 us (2%)
    pallas_call x1, Pallas kernels, local(): pl.pallas_call(kernel, out_shape=(jax.ShapeDtypeStruct((rows, picks), jnp...  34.5 us
    unnamed x2, local copies, waits for them, and re-layouts  1.11 us

profile of v4, /device:TPU:1, one launch (start us, length us, event | category | flops | bytes accessed | tf_op | source)
XLA Modules:
  0.0 36.3 jit_solution(13062811046396870686)
XLA Ops:
  0.6 34.5 %shard_map.59 = (f32[16,64]{1,0:T(8,128)S(1)}, f32[1,16]{1,0:T(1,128)S(1)}) custom-call(bf16[16,4096]{1,0:T(8,128)(2,1)} %x_ref.1, bf16[4096,2432]{1,0:T(8,128)(2,1)} %w_ref.1, s32[64,512]{1,0:T(8,128)} %bitcast.4, s32[1,512]{1,0:T(1,128)} %bitcast.5), custom_call_target="tpu_custom_call" | custom-call | tf_op jit(solution)/shard_map/pallas_call | solution.py:299
  35.2 0.6 %copy.8 = f32[16,64]{1,0:T(8,128)} copy(f32[16,64]{1,0:T(8,128)S(1)} %get-tuple-element.8) | data formatting | bytes 8192
  35.8 0.5 %copy.9 = f32[16]{0:T(128)} copy(f32[16]{0:T(128)S(1)} %bitcast.3) | data formatting | bytes 128
